TPU v7x, 32 devices: a whole 2x2x4 slice. The times are simulated.
32 devices in a mesh: seq: 8 (over y, x, core), stretch: 4 (over z).
Axes of the slice: x: 2, y: 2, z: 4, core: 2. Of those that a mesh axis runs over, the one named last changes fastest.
Arguments:
- queries: bfloat16 [4096, 1792], P(('stretch', 'seq')), may hold values from -140 to 140
- keys: bfloat16 [4096, 256], P(('stretch', 'seq')), may hold values from -6 to 6
- values: bfloat16 [4096, 256], P(('stretch', 'seq')), may hold values from -6 to 6
Outputs:
- attended: bfloat16 [4096, 1792], P(('stretch', 'seq'))
All inputs are finite; a program needn't handle non-finite values.
Results may differ from a plain program's by a relative error of at most 0.011.
Values may be sent and summed in bfloat16 or wider, within the bound.
A program may use at most 64 MiB of HBM per device.

v0:
```python
import math

import jax
import jax.numpy as jnp
from jax import lax
from jax.sharding import PartitionSpec as P

QUERY_HEADS = 14
KEY_VALUE_HEADS = 2
HEAD_SIZE = 128
BLOCKS = 4


def passed_along(array, axis, by):
    size = lax.axis_size(axis)
    pairs = [(i, i + by) for i in range(size) if 0 <= i + by < size]
    return lax.ppermute(array, axis, pairs)


def apply_rotary(rows, token_positions, heads):
    half_width = HEAD_SIZE // 2
    inverse = 10000000.0 ** (-(jnp.arange(half_width, dtype=jnp.float32) * 2.0) / HEAD_SIZE)
    angles = token_positions.astype(jnp.float32)[:, None] * inverse[None, :]
    cosine = jnp.cos(angles)[:, None, :]
    sine_part = jnp.sin(angles)[:, None, :]
    shaped = rows.reshape(rows.shape[0], heads, HEAD_SIZE).astype(jnp.float32)
    first_half = shaped[..., :half_width]
    second_half = shaped[..., half_width:]
    turned = jnp.concatenate(
        [
            first_half * cosine - second_half * sine_part,
            second_half * cosine + first_half * sine_part,
        ],
        axis=-1,
    )
    return turned.reshape(rows.shape[0], heads * HEAD_SIZE).astype(jnp.bfloat16)


def empty_state(count_of_rows):
    head_cluster = QUERY_HEADS // KEY_VALUE_HEADS
    return (
        jnp.full((KEY_VALUE_HEADS, head_cluster, count_of_rows), -1e30, jnp.float32),
        jnp.zeros((KEY_VALUE_HEADS, head_cluster, count_of_rows), jnp.float32),
        jnp.zeros((KEY_VALUE_HEADS, head_cluster, count_of_rows, HEAD_SIZE), jnp.float32),
    )


def attend(rotated_query, rows_of_keys, rows_of_values, block_count, key_span, causal):
    count_of_rows = rotated_query.shape[0]
    head_cluster = QUERY_HEADS // KEY_VALUE_HEADS
    grouped_queries = rotated_query.reshape(count_of_rows, KEY_VALUE_HEADS, head_cluster, HEAD_SIZE)
    score_scale = 1.0 / math.sqrt(HEAD_SIZE)

    def advance(block_number, state):
        running_max, running_sum, accumulated = state
        key_start = block_number * key_span
        key_block = lax.dynamic_slice_in_dim(rows_of_keys, key_start, key_span, 0)
        value_block = lax.dynamic_slice_in_dim(rows_of_values, key_start, key_span, 0)
        scores = (
            jnp.einsum(
                "rkgd,skd->kgrs", grouped_queries, key_block, preferred_element_type=jnp.float32
            )
            * score_scale
        )
        if causal is not None:
            allowed = (
                causal[:, None] >= (key_start + jnp.arange(key_span, dtype=jnp.int32))[None, :]
            )
            scores = jnp.where(allowed, scores, -1e30)
        new_max = jnp.maximum(running_max, jnp.max(scores, axis=-1))
        rescale = jnp.exp(running_max - new_max)
        weights = jnp.exp(scores - new_max[..., None])
        running_sum = running_sum * rescale + jnp.sum(weights, axis=-1)
        accumulated = accumulated * rescale[..., None] + jnp.einsum(
            "kgrs,skd->kgrd",
            weights.astype(jnp.bfloat16),
            value_block,
            preferred_element_type=jnp.float32,
        )
        return (new_max, running_sum, accumulated)

    return lax.fori_loop(0, block_count, advance, empty_state(count_of_rows))


def on_device(queries, keys, values):
    shard_rows = queries.shape[0]
    seq_count = lax.axis_size("seq")
    seq_index = lax.axis_index("seq")
    group_index = lax.axis_index("stretch")
    sequence_count = lax.axis_size("stretch") // BLOCKS
    block_length = shard_rows * seq_count
    local_block = group_index // sequence_count
    key_span = min(512, block_length)
    token_positions = seq_index * shard_rows + jnp.arange(shard_rows, dtype=jnp.int32)
    rotated_keys = apply_rotary(keys, token_positions, KEY_VALUE_HEADS)
    rows_of_keys, rows_of_values = (
        lax.all_gather(rotated_keys, "seq", axis=0, tiled=True),
        lax.all_gather(values, "seq", axis=0, tiled=True),
    )
    rows_of_keys = rows_of_keys.reshape(block_length, KEY_VALUE_HEADS, HEAD_SIZE)
    rows_of_values = rows_of_values.reshape(block_length, KEY_VALUE_HEADS, HEAD_SIZE)
    near_count = ((seq_index + 1) * shard_rows + key_span - 1) // key_span
    own_state = attend(
        apply_rotary(queries, token_positions, QUERY_HEADS),
        rows_of_keys,
        rows_of_values,
        near_count,
        key_span,
        token_positions,
    )

    def serve(incoming, offset, key_source, value_source):
        if offset == 1:
            query_place = token_positions + block_length
        else:
            query_place = jnp.full((shard_rows,), 2 * block_length - 1, jnp.int32)
        return attend(
            apply_rotary(incoming, query_place, QUERY_HEADS),
            key_source,
            value_source,
            block_length // key_span,
            key_span,
            None,
        )

    farthest = BLOCKS - 2
    pieces_list = [(own_state, True)]
    for offset in range(1, farthest + 1):
        visiting = passed_along(queries, "stretch", -offset * sequence_count)
        helping = local_block + offset < BLOCKS
        partial_state = lax.cond(
            helping,
            lambda incoming, offset=offset: serve(incoming, offset, rows_of_keys, rows_of_values),
            lambda incoming: empty_state(shard_rows),
            visiting,
        )
        returned_state = passed_along(partial_state, "stretch", offset * sequence_count)
        pieces_list.append((returned_state, local_block >= offset))
    far_rows, far_values = passed_along(
        (rows_of_keys, rows_of_values), "stretch", (BLOCKS - 1) * sequence_count
    )
    far_state = lax.cond(
        local_block >= BLOCKS - 1,
        lambda incoming: serve(incoming, BLOCKS - 1, far_rows, far_values),
        lambda incoming: empty_state(shard_rows),
        queries,
    )
    pieces_list.append((far_state, local_block >= BLOCKS - 1))
    cleaned = []
    for member, usable in pieces_list:
        cleaned.append(
            (
                jnp.where(usable, member[0], -1e30),
                jnp.where(usable, member[1], 0.0),
                jnp.where(usable, member[2], 0.0),
            )
        )
    overall_max = cleaned[0][0]
    for member in cleaned[1:]:
        overall_max = jnp.maximum(overall_max, member[0])
    numerator = jnp.zeros_like(cleaned[0][2])
    denominator = jnp.zeros_like(cleaned[0][1])
    for member in cleaned:
        weight_term = jnp.exp(member[0] - overall_max)
        numerator = numerator + member[2] * weight_term[..., None]
        denominator = denominator + member[1] * weight_term
    output = numerator / denominator[..., None]
    output = jnp.transpose(output, (2, 0, 1, 3)).reshape(shard_rows, QUERY_HEADS * HEAD_SIZE)
    return output.astype(jnp.bfloat16)


def solution(mesh):
    placed = (P(("stretch", "seq"), None), P(("stretch", "seq"), None), P(("stretch", "seq"), None))
    return jax.shard_map(
        on_device,
        mesh=mesh,
        in_specs=placed,
        out_specs=P(("stretch", "seq"), None),
        check_vma=False,
    )
```

profile of v0, /device:TPU:25, one launch (start us, length us, event | category | flops | bytes accessed | tf_op | source)
XLA Modules:
  0.0 129.7 jit_solution(7577735770510478455)
XLA Ops:
  1.2 10.5 %all_gather.6 = bf16[1024,256]{0,1:T(8,128)(2,1)S(1)} all-gather(bf16[128,256]{0,1:T(8,128)(2,1)S(1)} %bitcast.189), channel_id=1, replica_groups=mesh['seq'=8,'stretch'=4] {'seq'}, dimensions={0}, use_global_device_ids=true | all-gather | bytes 589824 | tf_op jit(solution)/shard_map/all_gather | solution.py:97
  13.0 2.0 %copy.26 = bf16[128,1792]{0,1:T(8,128)(2,1)} copy(bf16[128,1792]{1,0:T(8,128)(2,1)} %param.17) | data formatting | bytes 917504 | tf_op args[0]
  15.0 2.1 %collective-permute-start.2 = (bf16[128,1792]{0,1:T(8,128)(2,1)}, bf16[128,1792]{0,1:T(8,128)(2,1)}, u32[]{:S(2)}, u32[]{:S(2)}) collective-permute-start(bf16[128,1792]{0,1:T(8,128)(2,1)} %copy.26), channel_id=1, source_target_pairs={{2,0},{3,1},{6,4},{7,5},{10,8},{11,9},{14,12},{15,13},{18,16},{19,... | collective-permute-start | bytes 1376264 | tf_op jit(solution)/shard_map/ppermute | solution.py:17
  18.1 10.2 %all_gather.7 = bf16[1024,256]{0,1:T(8,128)(2,1)S(1)} all-gather(bf16[128,256]{0,1:T(8,128)(2,1)S(1)} %copy.27), channel_id=1, replica_groups=mesh['seq'=8,'stretch'=4] {'seq'}, dimensions={0}, use_global_device_ids=true | all-gather | bytes 589824 | tf_op jit(solution)/shard_map/all_gather | solution.py:98
  29.6 7.1 %collective-permute-start = (bf16[128,1792]{0,1:T(8,128)(2,1)}, bf16[128,1792]{0,1:T(8,128)(2,1)}, u32[]{:S(2)}, u32[]{:S(2)}) collective-permute-start(bf16[128,1792]{0,1:T(8,128)(2,1)} %copy.26), channel_id=1, source_target_pairs={{1,0},{2,1},{3,2},{5,4},{6,5},{7,6},{9,8},{10,9},{11,10},{13,12},{... | collective-permute-start | bytes 1376264 | tf_op jit(solution)/shard_map/ppermute | solution.py:17
  38.0 2.3 %conditional.4 = (f32[2,7,128]{2,1,0:T(8,128)}, f32[2,7,128]{2,1,0:T(8,128)}, f32[2,7,128,128]{3,2,1,0:T(8,128)}) conditional(s32[]{:T(128)} %convert_element_type.115, () %tuple.78, (bf16[128,1792]{0,1:T(8,128)(2,1)}, bf16[1024,2,128]{0,2,1:T(8,128)(2,1)S(1)}, bf16[1024,2,128]{0,2,1:T(8,128)(2,1)S(1)}) %tuple.196), branch_computations={%region_10.11_spmd, %region_11.16_spmd} | conditional | flops 479863808 | bytes 33213768 | solution.py:131
  41.9 2.4 %copy.43 = f32[2,7,128,128]{2,3,1,0:T(8,128)} copy(f32[2,7,128,128]{3,2,1,0:T(8,128)} %get-tuple-element.478) | data formatting | bytes 1835008 | tf_op jit(solution)/shard_map/cond | solution.py:131
  46.0 2.2 %conditional.3 = (f32[2,7,128]{2,1,0:T(8,128)}, f32[2,7,128]{2,1,0:T(8,128)}, f32[2,7,128,128]{3,2,1,0:T(8,128)}) conditional(s32[]{:T(128)} %convert_element_type.114, () %tuple.76, (bf16[128,1792]{0,1:T(8,128)(2,1)}, s32[128]{0:T(128)S(1)}, bf16[1024,2,128]{0,2,1:T(8,128)(2,1)S(1)}, bf16[1024,2,128]{0,2,1:T(8,128)(2,1)S(1)}) %tuple.197), branch_computations={%region_4.5_spmd, %region_5.10_spmd} | conditional | flops 479872192 | bytes 33345864 | solution.py:131
  48.2 2.4 %copy.42 = f32[2,7,128,128]{2,3,1,0:T(8,128)} copy(f32[2,7,128,128]{3,2,1,0:T(8,128)} %get-tuple-element.477) | data formatting | bytes 1835008 | tf_op jit(solution)/shard_map/cond | solution.py:131
  51.9 11.1 %collective-permute-done.9 = f32[2,7,128]{2,1,0:T(8,128)S(1)} collective-permute-done((f32[2,7,128]{2,1,0:T(8,128)}, f32[2,7,128]{2,1,0:T(8,128)S(1)}, u32[]{:S(2)}, u32[]{:S(2)}) %collective-permute-start.9) | collective-permute-done | bytes 7200 | tf_op jit(solution)/shard_map/ppermute | solution.py:17
  67.1 3.4 %while.69 = (s32[]{:T(128)}, f32[2,7,128]{2,1,0:T(8,128)S(1)}, f32[2,7,128]{2,1,0:T(8,128)S(1)}, f32[2,7,128,128]{3,2,1,0:T(8,128)S(1)}, s32[]{:T(128)}, /*index...) while((s32[]{:T(128)}, f32[2,7,128]{2,1,0:T(8,128)S(1)}, ...), condition=%wide.region_3.4_spmd.clone, body=%wide.region_0.3_spmd.clone.sunk | while | flops 480383104 | bytes 14212291 | solution.py:82
  69.0 1.4 %fusion.118 = f32[2,7,128,128]{3,2,1,0:T(8,128)S(1)} fusion(f32[2,512,128,7]{2,1,3,0:T(8,128)S(1)} %get-tuple-element.899, f32[2,7,128]{2,1,0:T(8,128)S(1)} %max.50, pred[128,512]{0,1:T(8,128)(4,1)S(1)} %broadcast_compare_fusion.2, f32[2,7,128,128]{3,2,1,0:T(8,128)S(1)} %get-tuple-element.1068, f32[2,7,128]{2,1,0:T(8,128)S(1)} %get-tuple-element.901, ...), kind=kOutput, calls=%fused_computation.11.clone.1 | convolution fusion | flops 239009792 | bytes 5849092 | tf_op jit(solution)/shard_map/while/body/kgrs,skd->kgrd/dot_general | solution.py:74
  70.8 23.1 %conditional.5 = (f32[2,7,128]{2,1,0:T(8,128)}, f32[2,7,128]{2,1,0:T(8,128)}, f32[2,7,128,128]{2,3,1,0:T(8,128)S(1)}) conditional(s32[]{:T(128)} %convert_element_type.116, () %tuple.80, (bf16[128,1792]{1,0:T(8,128)(2,1)}, bf16[1024,2,128]{0,2,1:T(8,128)(2,1)S(1)}, bf16[1024,2,128]{0,2,1:T(8,128)(2,1)}) %tuple.199), branch_computations={%region_16.17_spmd, %region_17.22_spmd} | conditional | flops 479863808 | bytes 35964232 | solution.py:142
  70.8 2.0 %copy.38 = bf16[128,1792]{0,1:T(8,128)(2,1)} copy(bf16[128,1792]{1,0:T(8,128)(2,1)} %get-tuple-element.615) | data formatting | bytes 917504 | tf_op jit(solution)/shard_map
  74.5 19.1 %while.68 = (s32[]{:T(128)}, f32[2,7,128]{2,1,0:T(8,128)}, f32[2,7,128]{2,1,0:T(8,128)}, f32[2,7,128,128]{3,2,1,0:T(8,128)S(1)}, bf16[1024,2,128]{0,2,1:T(8,128)...) while((s32[]{:T(128)}, f32[2,7,128]{2,1,0:T(8,128)}, ...), condition=%wide.region_21.21_spmd.clone, body=%wide.region_18.20_spmd.clone.sunk | while | flops 477799168 | bytes 28623056 | solution.py:82
  74.5 2.5 %bitcast_reduce_fusion.6 = (f32[2,7,128]{2,1,0:T(8,128)S(1)}, f32[2,512,128,7]{2,1,3,0:T(8,128)}) fusion(bf16[128,2,7,128]{3,0,2,1:T(8,128)(2,1)S(1)} %get-tuple-element.962, bf16[1024,2,128]{0,2,1:T(8,128)(2,1)S(1)} %get-tuple-element.961, s32[]{:T(128)S(6)} %select_n.172), kind=kOutput, calls=%fused_computation.84.clone.1 | convolution fusion | flops 236714240 | bytes 4398084 | tf_op jit(solution)/shard_map/cond/branch_1_fun/while/body/eval_jaxpr/rkgd,skd->kgrs/dot_general | solution.py:60
  77.0 2.8 %fusion.122 = f32[2,7,128]{2,1,0:T(8,128)S(1)} fusion(f32[2,512,128,7]{2,1,3,0:T(8,128)} %get-tuple-element.910, f32[2,7,128]{2,1,0:T(8,128)S(1)} %select_maximum_fusion.6), kind=kLoop, calls=%fused_computation.87.clone.1 | loop fusion | flops 2750720 | bytes 3684352 | tf_op jit(solution)/shard_map/cond/branch_1_fun/while/body/eval_jaxpr/reduce_sum | solution.py:73
  81.0 2.2 %fusion.124 = f32[2,7,128,128]{3,2,1,0:T(8,128)S(1)} fusion(f32[2,512,128,7]{2,1,3,0:T(8,128)S(1)} %copy-done.2, f32[2,7,128]{2,1,0:T(8,128)S(1)} %select_maximum_fusion.6, f32[2,7,128,128]{3,2,1,0:T(8,128)S(1)} %get-tuple-element.949, f32[2,7,128]{2,1,0:T(8,128)S(1)} %get-tuple-element.912, pred[]{:T(512)S(6)} %compare.12, ...), kind=kOutput, calls=%fused_computation.91.clone.1 | convolution fusion | flops 238321664 | bytes 5781509 | tf_op jit(solution)/shard_map/cond/branch_1_fun/while/body/eval_jaxpr/kgrs,skd->kgrd/dot_general | solution.py:74
  83.3 2.5 %bitcast_reduce_fusion.6 = (f32[2,7,128]{2,1,0:T(8,128)S(1)}, f32[2,512,128,7]{2,1,3,0:T(8,128)}) fusion(bf16[128,2,7,128]{3,0,2,1:T(8,128)(2,1)S(1)} %get-tuple-element.962, bf16[1024,2,128]{0,2,1:T(8,128)(2,1)S(1)} %get-tuple-element.961, s32[]{:T(128)S(6)} %select_n.172), kind=kOutput, calls=%fused_computation.84.clone.1 | convolution fusion | flops 236714240 | bytes 4398084 | tf_op jit(solution)/shard_map/cond/branch_1_fun/while/body/eval_jaxpr/rkgd,skd->kgrs/dot_general | solution.py:60
  86.6 2.8 %fusion.122 = f32[2,7,128]{2,1,0:T(8,128)S(1)} fusion(f32[2,512,128,7]{2,1,3,0:T(8,128)} %get-tuple-element.910, f32[2,7,128]{2,1,0:T(8,128)S(1)} %select_maximum_fusion.6), kind=kLoop, calls=%fused_computation.87.clone.1 | loop fusion | flops 2750720 | bytes 3684352 | tf_op jit(solution)/shard_map/cond/branch_1_fun/while/body/eval_jaxpr/reduce_sum | solution.py:73
  91.4 2.2 %fusion.124 = f32[2,7,128,128]{3,2,1,0:T(8,128)S(1)} fusion(f32[2,512,128,7]{2,1,3,0:T(8,128)S(1)} %copy-done.2, f32[2,7,128]{2,1,0:T(8,128)S(1)} %select_maximum_fusion.6, f32[2,7,128,128]{3,2,1,0:T(8,128)S(1)} %get-tuple-element.949, f32[2,7,128]{2,1,0:T(8,128)S(1)} %get-tuple-element.912, pred[]{:T(512)S(6)} %compare.12, ...), kind=kOutput, calls=%fused_computation.91.clone.1 | convolution fusion | flops 238321664 | bytes 5781509 | tf_op jit(solution)/shard_map/cond/branch_1_fun/while/body/eval_jaxpr/kgrs,skd->kgrd/dot_general | solution.py:74
  93.9 18.2 %collective-permute-done.8 = f32[2,7,128]{2,1,0:T(8,128)S(1)} collective-permute-done((f32[2,7,128]{2,1,0:T(8,128)}, f32[2,7,128]{2,1,0:T(8,128)S(1)}, u32[]{:S(2)}, u32[]{:S(2)}) %collective-permute-start.8) | collective-permute-done | bytes 7200 | tf_op jit(solution)/shard_map/ppermute | solution.py:17
  112.2 13.8 %collective-permute-done.3 = f32[2,7,128]{2,1,0:T(8,128)S(1)} collective-permute-done((f32[2,7,128]{2,1,0:T(8,128)}, f32[2,7,128]{2,1,0:T(8,128)S(1)}, u32[]{:S(2)}, u32[]{:S(2)}) %collective-permute-start.3) | collective-permute-done | bytes 7200 | tf_op jit(solution)/shard_map/ppermute | solution.py:17
  126.8 2.0 %divide_convert_fusion = bf16[2,7,128,128]{2,3,1,0:T(8,128)(2,1)S(1)} fusion(f32[2,7,128,128]{2,3,1,0:T(8,128)S(1)} %get-tuple-element.618, f32[2,7,128,128]{2,3,1,0:T(8,128)} %collective-permute-done.7, f32[2,7,128,128]{2,3,1,0:T(8,128)} %collective-permute-done.6, f32[2,7,128,128]{2,3,1,0:T(8,128)S(1)} %copy.41, f32[2,7,128]{2,1,0:T(8,128)S(1)} %get-tuple-element.687, ...), kind=kLoop, calls=%fused_computation.111 | loop fusion | flops 2752512 | bytes 4164611 | tf_op jit(solution)/shard_map/convert_element_type | solution.py:169
  (68 shorter events, 28.7 us)
Async XLA Ops:
  11.7 52.6 %collective-permute-start.4 = (bf16[1024,2,128]{0,2,1:T(8,128)(2,1)S(1)}, bf16[1024,2,128]{0,2,1:T(8,128)(2,1)S(1)}, u32[]{:S(2)}, u32[]{:S(2)}) collective-permute-start(bf16[1024,2,128]{0,2,1:T(8,128)(2,1)S(1)} %bitcast.174), channel_id=1, source_target_pairs={{0,3},{4,7},{8,11},{12,15},{16,19},{20,23},{24,27},{28,31}} | collective-permute-start | bytes 1572872 | tf_op jit(solution)/shard_map/ppermute | solution.py:17
  15.0 23.0 %collective-permute-start.2 = (bf16[128,1792]{0,1:T(8,128)(2,1)}, bf16[128,1792]{0,1:T(8,128)(2,1)}, u32[]{:S(2)}, u32[]{:S(2)}) collective-permute-start(bf16[128,1792]{0,1:T(8,128)(2,1)} %copy.26), channel_id=1, source_target_pairs={{2,0},{3,1},{6,4},{7,5},{10,8},{11,9},{14,12},{15,13},{18,16},{19,... | collective-permute-start | bytes 1376264 | tf_op jit(solution)/shard_map/ppermute | solution.py:17
  28.3 37.3 %collective-permute-start.5 = (bf16[1024,2,128]{0,2,1:T(8,128)(2,1)S(1)}, bf16[1024,2,128]{0,2,1:T(8,128)(2,1)S(1)}, u32[]{:S(2)}, u32[]{:S(2)}) collective-permute-start(bf16[1024,2,128]{0,2,1:T(8,128)(2,1)S(1)} %bitcast.178), channel_id=1, source_target_pairs={{0,3},{4,7},{8,11},{12,15},{16,19},{20,23},{24,27},{28,31}} | collective-permute-start | bytes 1572872 | tf_op jit(solution)/shard_map/ppermute | solution.py:17
  29.6 16.4 %collective-permute-start = (bf16[128,1792]{0,1:T(8,128)(2,1)}, bf16[128,1792]{0,1:T(8,128)(2,1)}, u32[]{:S(2)}, u32[]{:S(2)}) collective-permute-start(bf16[128,1792]{0,1:T(8,128)(2,1)} %copy.26), channel_id=1, source_target_pairs={{1,0},{2,1},{3,2},{5,4},{6,5},{7,6},{9,8},{10,9},{11,10},{13,12},{... | collective-permute-start | bytes 1376264 | tf_op jit(solution)/shard_map/ppermute | solution.py:17
  40.3 22.7 %collective-permute-start.9 = (f32[2,7,128]{2,1,0:T(8,128)}, f32[2,7,128]{2,1,0:T(8,128)S(1)}, u32[]{:S(2)}, u32[]{:S(2)}) collective-permute-start(f32[2,7,128]{2,1,0:T(8,128)} %get-tuple-element.482), channel_id=1, source_target_pairs={{0,2},{1,3},{4,6},{5,7},{8,10},{9,11},{12,14},{13,15},{16,18},{17,... | collective-permute-start | bytes 21512 | tf_op jit(solution)/shard_map/ppermute | solution.py:17
  44.3 82.4 %collective-permute-start.7 = (f32[2,7,128,128]{2,3,1,0:T(8,128)}, f32[2,7,128,128]{2,3,1,0:T(8,128)}, u32[]{:S(2)}, u32[]{:S(2)}) collective-permute-start(f32[2,7,128,128]{2,3,1,0:T(8,128)} %copy.43), channel_id=1, source_target_pairs={{0,2},{1,3},{4,6},{5,7},{8,10},{9,11},{12,14},{13,15},{16,18},{17,... | collective-permute-start | bytes 2752520 | tf_op jit(solution)/shard_map/ppermute | solution.py:17
  50.6 76.1 %collective-permute-start.6 = (f32[2,7,128,128]{2,3,1,0:T(8,128)}, f32[2,7,128,128]{2,3,1,0:T(8,128)}, u32[]{:S(2)}, u32[]{:S(2)}) collective-permute-start(f32[2,7,128,128]{2,3,1,0:T(8,128)} %copy.42), channel_id=1, source_target_pairs={{0,1},{1,2},{2,3},{4,5},{5,6},{6,7},{8,9},{9,10},{10,11},{12,13},{... | collective-permute-start | bytes 2752520 | tf_op jit(solution)/shard_map/ppermute | solution.py:17
  63.0 49.0 %collective-permute-start.8 = (f32[2,7,128]{2,1,0:T(8,128)}, f32[2,7,128]{2,1,0:T(8,128)S(1)}, u32[]{:S(2)}, u32[]{:S(2)}) collective-permute-start(f32[2,7,128]{2,1,0:T(8,128)} %get-tuple-element.481), channel_id=1, source_target_pairs={{0,1},{1,2},{2,3},{4,5},{5,6},{6,7},{8,9},{9,10},{10,11},{12,13},{... | collective-permute-start | bytes 21512 | tf_op jit(solution)/shard_map/ppermute | solution.py:17
  64.3 47.9 %collective-permute-start.1 = (f32[2,7,128]{2,1,0:T(8,128)}, f32[2,7,128]{2,1,0:T(8,128)S(1)}, u32[]{:S(2)}, u32[]{:S(2)}) collective-permute-start(f32[2,7,128]{2,1,0:T(8,128)} %get-tuple-element.474), channel_id=1, source_target_pairs={{0,1},{1,2},{2,3},{4,5},{5,6},{6,7},{8,9},{9,10},{10,11},{12,13},{... | collective-permute-start | bytes 21512 | tf_op jit(solution)/shard_map/ppermute | solution.py:17
  65.7 1.3 %copy-start.3 = (bf16[1024,2,128]{0,2,1:T(8,128)(2,1)}, bf16[1024,2,128]{0,2,1:T(8,128)(2,1)S(1)}, u32[]{:S(2)}) copy-start(bf16[1024,2,128]{0,2,1:T(8,128)(2,1)S(1)} %collective-permute-done.5) | copy-start | bytes 1572868
  65.7 60.3 %collective-permute-start.3 = (f32[2,7,128]{2,1,0:T(8,128)}, f32[2,7,128]{2,1,0:T(8,128)S(1)}, u32[]{:S(2)}, u32[]{:S(2)}) collective-permute-start(f32[2,7,128]{2,1,0:T(8,128)} %get-tuple-element.475), channel_id=1, source_target_pairs={{0,2},{1,3},{4,6},{5,7},{8,10},{9,11},{12,14},{13,15},{16,18},{17,... | collective-permute-start | bytes 21512 | tf_op jit(solution)/shard_map/ppermute | solution.py:17
  77.0 4.0 %copy-start.2 = (f32[2,512,128,7]{2,1,3,0:T(8,128)S(1)}, f32[2,512,128,7]{2,1,3,0:T(8,128)}, u32[]{:S(2)}) copy-start(f32[2,512,128,7]{2,1,3,0:T(8,128)} %get-tuple-element.910) | copy-start | bytes 11010052 | tf_op jit(solution)/shard_map/cond/branch_1_fun/while
  85.8 5.6 %copy-start.2 = (f32[2,512,128,7]{2,1,3,0:T(8,128)S(1)}, f32[2,512,128,7]{2,1,3,0:T(8,128)}, u32[]{:S(2)}) copy-start(f32[2,512,128,7]{2,1,3,0:T(8,128)} %get-tuple-element.910) | copy-start | bytes 11010052 | tf_op jit(solution)/shard_map/cond/branch_1_fun/while
where the time goes:
time: 131 us; the launch traced here: 130 us
  waiting for transfers between devices  43.6 us (33%)
  blocking collectives  20.8 us (16%)
  starting transfers between devices  19.5 us (15%)
  local copies, waits for them, and re-layouts  18.6 us (14%)
  other arithmetic  15 us (11%)
  matrix products  11.6 us (9%)
    ppermute x10, waiting for transfers between devices, passed_along(): return lax.ppermute(array, axis, pairs)  43.6 us
    ppermute x10, starting transfers between devices, passed_along(): return lax.ppermute(array, axis, pairs)  19.5 us
    all_gather x1, blocking collectives, on_device(): lax.all_gather(rotated_keys, 'seq', axis=0, tiled=True)  10.5 us
    all_gather x1, blocking collectives, on_device(): lax.all_gather(values, 'seq', axis=0, tiled=True)  10.2 us
    another operation x10, local copies, waits for them, and re-layouts  6.56 us
    reduce_sum x3, other arithmetic, advance(): running_sum = running_sum * rescale + jnp.sum(weights, axis=-1)  6.38 us
    dot_general x3, matrix products, advance(): jnp.einsum('kgrs,skd->kgrd', weights.astype(jnp.bfloat16), value_block, p...  5.85 us
    dot_general x3, matrix products, advance(): jnp.einsum('rkgd,skd->kgrs', grouped_queries, key_block, preferred_elemen...  5.73 us
  transfers between devices with their start and end apart: 10, of which 5 were waited for; matrix products, arithmetic and copies ran while one was open for 32% of the time, Pallas kernels for 0%

commit v1 on v0

v1 whole, which is shorter than its diff:
```python
import functools
import math

import jax
import jax.numpy as jnp
import numpy as np
from jax import lax
from jax.experimental import pallas as pl
from jax.experimental.pallas import tpu as pltpu
from jax.sharding import PartitionSpec as P

QUERY_HEADS = 14
KEY_VALUE_HEADS = 2
HEAD_SIZE = 128
BLOCKS = 4
CLUSTER = QUERY_HEADS // KEY_VALUE_HEADS
WIDTH = CLUSTER * HEAD_SIZE
SCALE = math.log2(math.e) / math.sqrt(HEAD_SIZE)


def rotary_table(positions):
    half = HEAD_SIZE // 2
    inverse = 10000000.0 ** (-(np.arange(half, dtype=np.float64) * 2.0) / HEAD_SIZE)
    angles = np.arange(positions, dtype=np.float64)[:, None] * inverse[None, :]
    return np.concatenate([np.cos(angles), np.sin(angles)], axis=1).astype(np.float32)


def factors(table):
    swapped = pltpu.roll(table, HEAD_SIZE // 2, 1)
    low = lax.broadcasted_iota(jnp.int32, table.shape, 1) < HEAD_SIZE // 2
    return jnp.where(low, table, swapped), jnp.where(low, -swapped, table)


def turned(rows, cosine, sine):
    x = rows.astype(jnp.float32)
    return (x * cosine + pltpu.roll(x, HEAD_SIZE // 2, 1) * sine).astype(jnp.bfloat16)


def kernel(
    shape, q_in, k_in, v_in, table_in, out,
    q_raw, q_rot, kv, k_rot, table, table_next, table_far, peak, total, acc, o_buf,
    local_sem, pair_send, pair_recv, slot_recv, chain_send, flat_send, relay_send,
    out_local, out_send, out_recv,
):
    shard, pairs, side_a, side_b, sequences, span = shape
    rows = 2 * shard
    length = pairs * rows
    s = lax.axis_index("seq")
    g = lax.axis_index("stretch")
    h = s % 2
    p = s // 2
    a = p // side_b
    b = p % side_b
    n = g // sequences
    partner = {"seq": s + 1 - 2 * h}
    above = {"stretch": g + sequences}
    below = {"stretch": g - sequences}
    mesh_type = pl.DeviceIdType.MESH

    def pair_at(a_index, b_index):
        return a_index * side_b + b_index

    def device_at(pair):
        return {"seq": 2 * pair + h}

    a_peers = [pair_at((a + j) % side_a, b) for j in range(1, side_a)]
    b_peers = [pair_at(a, (b + j) % side_b) for j in range(1, side_b)]
    diagonal = [
        pair_at((a + i) % side_a, (b + j) % side_b)
        for i in range(1, side_a)
        for j in range(1, side_b)
    ]

    def at(start, size, unit):
        return pl.ds(pl.multiple_of(start, unit), size)

    mine = at(h * shard, shard, shard)
    own_rows = at(p * rows + h * shard, shard, shard)

    def head_columns(head):
        return at(head * HEAD_SIZE, HEAD_SIZE, HEAD_SIZE)

    local = [
        (k_in.at[:, head_columns(h)], kv.at[0, 0, own_rows, :]),
        (v_in.at[:, head_columns(h)], kv.at[1, 0, own_rows, :]),
        (q_in.at[:, at(h * WIDTH, WIDTH, HEAD_SIZE)], q_raw.at[mine, :]),
        (table_in.at[pl.ds(0, length), :], table),
        (table_in.at[at(length + p * rows, rows, rows), :], table_next),
        (table_in.at[pl.ds(2 * length - 8, 8), :], table_far),
    ]
    local = [
        pltpu.make_async_copy(src, dst, local_sem.at[i]) for i, (src, dst) in enumerate(local)
    ]
    for copy in local:
        copy.start()

    barrier = pltpu.get_barrier_semaphore()

    def greet(device):
        pl.semaphore_signal(barrier, inc=1, device_id=device, device_id_type=mesh_type)

    greet(partner)
    for peer in a_peers + b_peers:
        greet(device_at(peer))

    @pl.when(n < BLOCKS - 1)
    def _():
        greet(above)

    @pl.when(n > 0)
    def _():
        greet(below)

    pl.semaphore_wait(
        barrier,
        1 + len(a_peers) + len(b_peers) + jnp.minimum(n, 1) + jnp.minimum(BLOCKS - 1 - n, 1),
    )

    swap = [
        (k_in.at[:, head_columns(1 - h)], kv.at[0, 0, own_rows, :]),
        (v_in.at[:, head_columns(1 - h)], kv.at[1, 0, own_rows, :]),
        (q_in.at[:, at((1 - h) * WIDTH, WIDTH, HEAD_SIZE)], q_raw.at[mine, :]),
    ]
    swap = [
        pltpu.make_async_remote_copy(
            src_ref=src, dst_ref=dst, send_sem=pair_send.at[i], recv_sem=pair_recv.at[i],
            device_id=partner, device_id_type=mesh_type,
        )
        for i, (src, dst) in enumerate(swap)
    ]
    for copy in swap:
        copy.start()

    def slot(t, d, pair):
        return kv.at[t, d, at(pair * rows, rows, rows), :]

    def message(t, d, pair, device, d_to, send_sem):
        return pltpu.make_async_remote_copy(
            src_ref=slot(t, d, pair), dst_ref=slot(t, d_to, pair),
            send_sem=send_sem, recv_sem=slot_recv.at[t, d_to, pair],
            device_id=device, device_id_type=mesh_type,
        )

    def arrived(t, d, pair):
        message(t, d, pair, partner, d, chain_send.at[0, 0]).wait_recv()

    def chain(t, d):
        return message(t, d, p, above, d + 1, chain_send.at[t, d])

    def flat(t, d):
        return [
            message(t, d, p, device_at(peer), d, flat_send.at[t, d, i])
            for i, peer in enumerate(b_peers + a_peers)
        ]

    def relays(t, d):
        sources, targets = (b_peers, a_peers) if t == 0 else (a_peers, b_peers)
        return [
            [
                message(t, d, source, device_at(target), d, relay_send.at[t, d, i, j])
                for j, target in enumerate(targets)
            ]
            for i, source in enumerate(sources)
        ]

    def column(d, first):
        for t in range(2):
            if first:
                local[t].wait()
                swap[t].wait_recv()
            else:
                arrived(t, d, p)

            @pl.when(n < BLOCKS - 1)
            def _():
                chain(t, d).start()

            for copy in flat(t, d):
                copy.start()

    def spread(d):
        for t, sources in ((0, b_peers), (1, a_peers)):
            for source, copies in zip(sources, relays(t, d)):
                arrived(t, d, source)
                for copy in copies:
                    copy.start()

    def settle(d):
        for t, sources in ((0, a_peers), (1, b_peers)):
            for source in sources + diagonal:
                arrived(t, d, source)

    def rotate_queries(cosine, sine):
        for c in range(CLUSTER):
            q_rot[c] = turned(q_raw[:, c * HEAD_SIZE : (c + 1) * HEAD_SIZE], cosine, sine)

    def rotate_keys(d):
        def tile(i, carry):
            where = at(i * rows, rows, rows)
            cosine, sine = factors(table[where, :])
            k_rot[where, :] = turned(kv[0, d, where, :], cosine, sine)
            return carry

        lax.fori_loop(0, pairs, tile, 0)

    def attend(d, causal):
        def step(group, carry):
            where = at(group * span, span, span)

            def head(c, inner):
                scores = lax.dot_general(
                    q_rot[c], k_rot[where, :], (((1,), (1,)), ((), ())),
                    preferred_element_type=jnp.float32,
                )
                if causal:
                    row = p * rows + lax.broadcasted_iota(jnp.int32, scores.shape, 0)
                    key = group * span + lax.broadcasted_iota(jnp.int32, scores.shape, 1)
                    scores = jnp.where(row >= key, scores, -1e30)
                old = peak[c]
                new = jnp.maximum(old, jnp.max(scores, axis=1, keepdims=True) * SCALE)
                peak[c] = new
                fade = jnp.exp2(old - new)
                top = new[:, :1]
                weights = jnp.exp2(scores * SCALE - top)
                part = weights[:, :HEAD_SIZE]
                for i in range(1, span // HEAD_SIZE):
                    part = part + weights[:, i * HEAD_SIZE : (i + 1) * HEAD_SIZE]
                total[c] = total[c] * fade + part
                acc[c] = acc[c] * fade + jnp.dot(
                    weights.astype(jnp.bfloat16), kv[1, d, where, :],
                    preferred_element_type=jnp.float32,
                )
                return inner

            lax.fori_loop(0, CLUSTER, head, 0)
            return carry

        lax.fori_loop(0, length // span, step, 0)

    column(0, True)
    peak[...] = jnp.full(peak.shape, -1e30, jnp.float32)
    total[...] = jnp.zeros(total.shape, jnp.float32)
    acc[...] = jnp.zeros(acc.shape, jnp.float32)
    for copy in local[2:]:
        copy.wait()
    swap[2].wait_recv()
    rotate_queries(*factors(table[at(p * rows, rows, rows), :]))
    spread(0)

    @pl.when(n > 0)
    def _():
        column(1, False)

    settle(0)
    rotate_keys(0)
    attend(0, True)

    def earlier(d, carry):
        @pl.when(d == 1)
        def _():
            rotate_queries(*factors(table_next[...]))

        @pl.when(d == 2)
        def _():
            cosine, sine = factors(table_far[...])
            rotate_queries(
                jnp.broadcast_to(cosine[7:8], (rows, HEAD_SIZE)),
                jnp.broadcast_to(sine[7:8], (rows, HEAD_SIZE)),
            )

        spread(d)

        @pl.when(d < n)
        def _():
            column(d + 1, False)

        settle(d)
        rotate_keys(d)
        attend(d, False)
        return carry

    lax.fori_loop(1, n + 1, earlier, 0)

    theirs = at((1 - h) * shard, shard, shard)

    def results(c):
        where = head_columns(h * CLUSTER + c)
        return (
            pltpu.make_async_copy(o_buf.at[c, mine, :], out.at[:, where], out_local.at[c]),
            pltpu.make_async_remote_copy(
                src_ref=o_buf.at[c, theirs, :], dst_ref=out.at[:, where],
                send_sem=out_send.at[c], recv_sem=out_recv.at[c],
                device_id=partner, device_id_type=mesh_type,
            ),
        )

    for c in range(CLUSTER + 1):
        if c < CLUSTER:
            under = jnp.sum(total[c], axis=1, keepdims=True)
            o_buf[c] = (acc[c] / under).astype(jnp.bfloat16)
        if c > 0:
            for copy in results(c - 1):
                copy.start()

    for copy in swap:
        copy.wait_send()

    def sent(d, carry):
        for t in range(2):
            @pl.when(n < BLOCKS - 1)
            def _():
                chain(t, d).wait_send()

            for copy in flat(t, d):
                copy.wait_send()
            for copies in relays(t, d):
                for copy in copies:
                    copy.wait_send()
        return carry

    lax.fori_loop(0, n + 1, sent, 0)
    for c in range(CLUSTER):
        here, there = results(c)
        here.wait()
        there.wait_send()
        there.wait_recv()


def on_device(queries, keys, values):
    shard = queries.shape[0]
    pairs = lax.axis_size("seq") // 2
    sequences = lax.axis_size("stretch") // BLOCKS
    side_a = max(i for i in range(1, pairs + 1) if pairs % i == 0 and i * i <= pairs)
    side_b = pairs // side_a
    rows = 2 * shard
    length = pairs * rows
    span = math.gcd(1024, length)
    shape = (shard, pairs, side_a, side_b, sequences, span)
    table = jnp.asarray(rotary_table(2 * length))
    dma = pltpu.SemaphoreType.DMA
    peers = max(side_a - 1 + side_b - 1, 1)
    most = max(side_b - 1, side_a - 1, 1)
    return pl.pallas_call(
        functools.partial(kernel, shape),
        out_shape=jax.ShapeDtypeStruct(queries.shape, jnp.bfloat16),
        in_specs=[pl.BlockSpec(memory_space=pl.ANY)] * 4,
        out_specs=pl.BlockSpec(memory_space=pl.ANY),
        scratch_shapes=[
            pltpu.VMEM((rows, WIDTH), jnp.bfloat16),
            pltpu.VMEM((CLUSTER, rows, HEAD_SIZE), jnp.bfloat16),
            pltpu.VMEM((2, BLOCKS, length, HEAD_SIZE), jnp.bfloat16),
            pltpu.VMEM((length, HEAD_SIZE), jnp.bfloat16),
            pltpu.VMEM((length, HEAD_SIZE), jnp.float32),
            pltpu.VMEM((rows, HEAD_SIZE), jnp.float32),
            pltpu.VMEM((8, HEAD_SIZE), jnp.float32),
            pltpu.VMEM((CLUSTER, rows, HEAD_SIZE), jnp.float32),
            pltpu.VMEM((CLUSTER, rows, HEAD_SIZE), jnp.float32),
            pltpu.VMEM((CLUSTER, rows, HEAD_SIZE), jnp.float32),
            pltpu.VMEM((CLUSTER, rows, HEAD_SIZE), jnp.bfloat16),
            dma((6,)),
            dma((3,)),
            dma((3,)),
            dma((2, BLOCKS, pairs)),
            dma((2, BLOCKS)),
            dma((2, BLOCKS, peers)),
            dma((2, BLOCKS, most, most)),
            dma((CLUSTER,)),
            dma((CLUSTER,)),
            dma((CLUSTER,)),
        ],
        compiler_params=pltpu.CompilerParams(
            collective_id=0, has_side_effects=True, vmem_limit_bytes=60 * 1024 * 1024
        ),
    )(queries, keys, values, table)


def solution(mesh):
    placed = P(("stretch", "seq"), None)
    return jax.shard_map(
        on_device, mesh=mesh, in_specs=(placed,) * 3, out_specs=placed, check_vma=False
    )
```

time: 131 us -> 52.8 us (0.40)
  Pallas kernels: 0 us -> 50.9 us
  waiting for transfers between devices: 43.6 us -> 0 us
  blocking collectives: 20.8 us -> 0 us
  starting transfers between devices: 19.5 us -> 0 us
  local copies, waits for them, and re-layouts: 18.6 us -> 1.82 us
  other arithmetic: 15 us -> 0 us
  matrix products: 11.6 us -> 0 us
    pallas_call x0 -> x1, Pallas kernels: none -> 50.9 us  [on_device(): pl.pallas_call(functools.partial(kernel, shape), out_shape=jax.ShapeDtype...]
    ppermute x10 -> x0, waiting for transfers between devices: 43.6 us -> none  [passed_along(): return lax.ppermute(array, axis, pairs)]
    all_gather x2 -> x0, blocking collectives: 20.8 us -> none  [the longest x1 10.5 us: on_device(): lax.all_gather(rotated_keys, 'seq', axis=0, tiled=True)]
    ppermute x10 -> x0, starting transfers between devices: 19.5 us -> none  [passed_along(): return lax.ppermute(array, axis, pairs)]
    dot_general x6 -> x0, matrix products: 11.6 us -> none  [the longest x3 5.85 us: advance(): jnp.einsum('kgrs,skd->kgrd', weights.astype(jnp.bfloat16), value_block, p...]
    another operation x10 -> x0, local copies, waits for them, and re-layouts: 6.56 us -> none
    reduce_sum x3 -> x0, other arithmetic: 6.38 us -> none  [advance(): running_sum = running_sum * rescale + jnp.sum(weights, axis=-1)]
    cond x4 -> x0, local copies, waits for them, and re-layouts: 5.42 us -> none  [the longest x2 4.85 us: on_device(): lax.cond(helping, lambda incoming, offset=offset: serve(incoming, offset,...]
  transfers between devices with their start and end apart: 10 -> 0, of which waited for: 5 -> 0; matrix products, arithmetic and copies ran while one was open for 32% -> 0% of each run, Pallas kernels for 0% -> 0%
where the time goes in v1:
time: 52.8 us; the launch traced here: 52.7 us
  Pallas kernels  50.9 us (96%)
  local copies, waits for them, and re-layouts  1.82 us (3%)
    pallas_call x1, Pallas kernels, on_device(): pl.pallas_call(functools.partial(kernel, shape), out_shape=jax.ShapeDtype...  50.9 us
    unnamed x1, local copies, waits for them, and re-layouts  1.82 us

profile of v1, /device:TPU:25, one launch (start us, length us, event | category | flops | bytes accessed | tf_op | source)
XLA Modules:
  0.0 52.7 jit_solution(15540931889375878796)
XLA Ops:
  0.0 50.9 %shard_map.46 = bf16[128,1792]{1,0:T(8,128)(2,1)} custom-call(bf16[128,1792]{1,0:T(8,128)(2,1)} %q_in.1, bf16[128,256]{1,0:T(8,128)(2,1)} %k_in.1, bf16[128,256]{1,0:T(8,128)(2,1)} %v_in.1, f32[2048,128]{1,0:T(8,128)} %constant.2.clone.table_in), custom_call_target="tpu_custom_call" | custom-call | tf_op jit(solution)/shard_map/pallas_call | solution.py:343
  50.9 1.8 %copy.6 = bf16[128,1792]{1,0:T(8,128)(2,1)} copy(bf16[128,1792]{1,0:T(8,128)(2,1)} %shard_map.46) | data formatting | bytes 917504

commit v2 on v1

--- a/solution.py
+++ b/solution.py
@@ -15,6 +15,7 @@
 BLOCKS = 4
 CLUSTER = QUERY_HEADS // KEY_VALUE_HEADS
 WIDTH = CLUSTER * HEAD_SIZE
+UNROLL = CLUSTER
 SCALE = math.log2(math.e) / math.sqrt(HEAD_SIZE)
 
 
@@ -53,8 +54,10 @@
     b = p % side_b
     n = g // sequences
     partner = {"seq": s + 1 - 2 * h}
-    above = {"stretch": g + sequences}
-    below = {"stretch": g - sequences}
+
+    def block_at(shift):
+        return {"stretch": g + shift * sequences}
+
     mesh_type = pl.DeviceIdType.MESH
 
     def pair_at(a_index, b_index):
@@ -103,18 +106,16 @@
     for peer in a_peers + b_peers:
         greet(device_at(peer))
 
-    @pl.when(n < BLOCKS - 1)
-    def _():
-        greet(above)
-
-    @pl.when(n > 0)
-    def _():
-        greet(below)
-
-    pl.semaphore_wait(
-        barrier,
-        1 + len(a_peers) + len(b_peers) + jnp.minimum(n, 1) + jnp.minimum(BLOCKS - 1 - n, 1),
-    )
+    for k in range(1, BLOCKS):
+        @pl.when(n + k < BLOCKS)
+        def _():
+            greet(block_at(k))
+
+        @pl.when(n >= k)
+        def _():
+            greet(block_at(-k))
+
+    pl.semaphore_wait(barrier, len(a_peers) + len(b_peers) + BLOCKS)
 
     swap = [
         (k_in.at[:, head_columns(1 - h)], kv.at[0, 0, own_rows, :]),
@@ -144,8 +145,8 @@
     def arrived(t, d, pair):
         message(t, d, pair, partner, d, chain_send.at[0, 0]).wait_recv()
 
-    def chain(t, d):
-        return message(t, d, p, above, d + 1, chain_send.at[t, d])
+    def lift(t, k):
+        return message(t, 0, p, block_at(k), k, chain_send.at[t, k])
 
     def flat(t, d):
         return [
@@ -171,9 +172,11 @@
             else:
                 arrived(t, d, p)
 
-            @pl.when(n < BLOCKS - 1)
-            def _():
-                chain(t, d).start()
+            if first:
+                for k in range(BLOCKS - 1, 0, -1):
+                    @pl.when(n + k < BLOCKS)
+                    def _():
+                        lift(t, k).start()
 
             for copy in flat(t, d):
                 copy.start()
@@ -184,102 +187,106 @@
                 arrived(t, d, source)
                 for copy in copies:
                     copy.start()
+        for t, sources in ((1, b_peers), (0, a_peers)):
+            for source in sources:
+                arrived(t, d, source)
 
     def settle(d):
-        for t, sources in ((0, a_peers), (1, b_peers)):
-            for source in sources + diagonal:
+        for t in range(2):
+            for source in diagonal:
                 arrived(t, d, source)
 
-    def rotate_queries(cosine, sine):
+    def rotate_queries(version, cosine, sine):
         for c in range(CLUSTER):
-            q_rot[c] = turned(q_raw[:, c * HEAD_SIZE : (c + 1) * HEAD_SIZE], cosine, sine)
-
-    def rotate_keys(d):
-        def tile(i, carry):
-            where = at(i * rows, rows, rows)
-            cosine, sine = factors(table[where, :])
-            k_rot[where, :] = turned(kv[0, d, where, :], cosine, sine)
-            return carry
-
-        lax.fori_loop(0, pairs, tile, 0)
-
-    def attend(d, causal):
-        def step(group, carry):
-            where = at(group * span, span, span)
-
-            def head(c, inner):
-                scores = lax.dot_general(
-                    q_rot[c], k_rot[where, :], (((1,), (1,)), ((), ())),
-                    preferred_element_type=jnp.float32,
-                )
-                if causal:
-                    row = p * rows + lax.broadcasted_iota(jnp.int32, scores.shape, 0)
-                    key = group * span + lax.broadcasted_iota(jnp.int32, scores.shape, 1)
-                    scores = jnp.where(row >= key, scores, -1e30)
+            q_rot[version, c] = turned(
+                q_raw[:, c * HEAD_SIZE : (c + 1) * HEAD_SIZE], cosine, sine
+            )
+
+    def attend(d, line, causal):
+        where = at(line * span, span, span)
+        version = jnp.minimum(d, 2)
+        for i in range(side_b):
+            tile = at(line * span + i * rows, rows, rows)
+            cosine, sine = factors(table[tile, :])
+            k_rot[i * rows : (i + 1) * rows, :] = turned(kv[0, d, tile, :], cosine, sine)
+
+        def head(c, inner):
+            scores = lax.dot_general(
+                q_rot[version, c], k_rot[...], (((1,), (1,)), ((), ())),
+                preferred_element_type=jnp.float32,
+            )
+            if causal:
+                row = b * rows + lax.broadcasted_iota(jnp.int32, scores.shape, 0)
+                key = lax.broadcasted_iota(jnp.int32, scores.shape, 1)
+                scores = jnp.where(row >= key, scores, -1e30)
+            new = jnp.max(scores, axis=1, keepdims=True) * SCALE
+            if not causal:
                 old = peak[c]
-                new = jnp.maximum(old, jnp.max(scores, axis=1, keepdims=True) * SCALE)
+                new = jnp.maximum(old, new)
+                fade = jnp.exp2(old - new)
                 peak[c] = new
-                fade = jnp.exp2(old - new)
-                top = new[:, :1]
-                weights = jnp.exp2(scores * SCALE - top)
-                part = weights[:, :HEAD_SIZE]
-                for i in range(1, span // HEAD_SIZE):
-                    part = part + weights[:, i * HEAD_SIZE : (i + 1) * HEAD_SIZE]
-                total[c] = total[c] * fade + part
-                acc[c] = acc[c] * fade + jnp.dot(
-                    weights.astype(jnp.bfloat16), kv[1, d, where, :],
-                    preferred_element_type=jnp.float32,
-                )
-                return inner
-
-            lax.fori_loop(0, CLUSTER, head, 0)
-            return carry
-
-        lax.fori_loop(0, length // span, step, 0)
+                new = new[:, :1]
+            else:
+                peak[c] = jnp.broadcast_to(new, (rows, HEAD_SIZE))
+            weights = jnp.exp2(scores * SCALE - new)
+            part = weights[:, :HEAD_SIZE]
+            for i in range(1, span // HEAD_SIZE):
+                part = part + weights[:, i * HEAD_SIZE : (i + 1) * HEAD_SIZE]
+            product = jnp.dot(
+                weights.astype(jnp.bfloat16), kv[1, d, where, :],
+                preferred_element_type=jnp.float32,
+            )
+            total[c] = part if causal else total[c] * fade + part
+            acc[c] = product if causal else acc[c] * fade + product
+            return inner
+
+        lax.fori_loop(0, CLUSTER, head, 0, unroll=UNROLL)
 
     column(0, True)
-    peak[...] = jnp.full(peak.shape, -1e30, jnp.float32)
-    total[...] = jnp.zeros(total.shape, jnp.float32)
-    acc[...] = jnp.zeros(acc.shape, jnp.float32)
     for copy in local[2:]:
         copy.wait()
     swap[2].wait_recv()
-    rotate_queries(*factors(table[at(p * rows, rows, rows), :]))
+    rotate_queries(0, *factors(table[at(p * rows, rows, rows), :]))
     spread(0)
 
     @pl.when(n > 0)
     def _():
         column(1, False)
 
-    settle(0)
-    rotate_keys(0)
-    attend(0, True)
-
-    def earlier(d, carry):
-        @pl.when(d == 1)
+    attend(0, a, True)
+    rotate_queries(1, *factors(table_next[...]))
+    cosine, sine = factors(table_far[...])
+    rotate_queries(
+        2,
+        jnp.broadcast_to(cosine[7:8], (rows, HEAD_SIZE)),
+        jnp.broadcast_to(sine[7:8], (rows, HEAD_SIZE)),
+    )
+
+    def block(d, carry):
+        @pl.when(d + 1 <= n)
         def _():
-            rotate_queries(*factors(table_next[...]))
-
-        @pl.when(d == 2)
+            spread(d + 1)
+
+        @pl.when(d + 2 <= n)
         def _():
-            cosine, sine = factors(table_far[...])
-            rotate_queries(
-                jnp.broadcast_to(cosine[7:8], (rows, HEAD_SIZE)),
-                jnp.broadcast_to(sine[7:8], (rows, HEAD_SIZE)),
-            )
-
-        spread(d)
-
-        @pl.when(d < n)
-        def _():
-            column(d + 1, False)
+            column(d + 2, False)
 
         settle(d)
-        rotate_keys(d)
-        attend(d, False)
+
+        def visit(i, inner):
+            line = (a + i) % side_a
+            ahead = d + i // side_a
+
+            @pl.when((ahead <= n) & ((d > 0) | (i == side_a) | (line < a)))
+            def _():
+                attend(ahead, line, False)
+
+            return inner
+
+        lax.fori_loop(1, side_a + 1, visit, 0)
         return carry
 
-    lax.fori_loop(1, n + 1, earlier, 0)
+    lax.fori_loop(0, n + 1, block, 0)
 
     theirs = at((1 - h) * shard, shard, shard)
 
@@ -307,10 +314,6 @@
 
     def sent(d, carry):
         for t in range(2):
-            @pl.when(n < BLOCKS - 1)
-            def _():
-                chain(t, d).wait_send()
-
             for copy in flat(t, d):
                 copy.wait_send()
             for copies in relays(t, d):
@@ -319,6 +322,12 @@
         return carry
 
     lax.fori_loop(0, n + 1, sent, 0)
+    for t in range(2):
+        for k in range(1, BLOCKS):
+            @pl.when(n + k < BLOCKS)
+            def _():
+                lift(t, k).wait_send()
+
     for c in range(CLUSTER):
         here, there = results(c)
         here.wait()
@@ -334,7 +343,7 @@
     side_b = pairs // side_a
     rows = 2 * shard
     length = pairs * rows
-    span = math.gcd(1024, length)
+    span = side_b * rows
     shape = (shard, pairs, side_a, side_b, sequences, span)
     table = jnp.asarray(rotary_table(2 * length))
     dma = pltpu.SemaphoreType.DMA
@@ -347,9 +356,9 @@
         out_specs=pl.BlockSpec(memory_space=pl.ANY),
         scratch_shapes=[
             pltpu.VMEM((rows, WIDTH), jnp.bfloat16),
-            pltpu.VMEM((CLUSTER, rows, HEAD_SIZE), jnp.bfloat16),
+            pltpu.VMEM((3, CLUSTER, rows, HEAD_SIZE), jnp.bfloat16),
             pltpu.VMEM((2, BLOCKS, length, HEAD_SIZE), jnp.bfloat16),
-            pltpu.VMEM((length, HEAD_SIZE), jnp.bfloat16),
+            pltpu.VMEM((span, HEAD_SIZE), jnp.bfloat16),
             pltpu.VMEM((length, HEAD_SIZE), jnp.float32),
             pltpu.VMEM((rows, HEAD_SIZE), jnp.float32),
             pltpu.VMEM((8, HEAD_SIZE), jnp.float32),

time: 52.8 us -> 43 us (0.81)
  Pallas kernels: 50.9 us -> 41 us
    pallas_call x1, Pallas kernels: 50.9 us -> 41 us  [on_device(): pl.pallas_call(functools.partial(kernel, shape), out_shape=jax.ShapeDtype...]
where the time goes in v2:
time: 43 us; the launch traced here: 42.8 us
  Pallas kernels  41 us (95%)
  local copies, waits for them, and re-layouts  1.82 us (4%)
    pallas_call x1, Pallas kernels, on_device(): pl.pallas_call(functools.partial(kernel, shape), out_shape=jax.ShapeDtype...  41 us
    unnamed x1, local copies, waits for them, and re-layouts  1.82 us

profile of v2, /device:TPU:25, one launch (start us, length us, event | category | flops | bytes accessed | tf_op | source)
XLA Modules:
  0.0 42.8 jit_solution(7316543970492080884)
XLA Ops:
  0.0 41.0 %shard_map.46 = bf16[128,1792]{1,0:T(8,128)(2,1)} custom-call(bf16[128,1792]{1,0:T(8,128)(2,1)} %q_in.1, bf16[128,256]{1,0:T(8,128)(2,1)} %k_in.1, bf16[128,256]{1,0:T(8,128)(2,1)} %v_in.1, f32[2048,128]{1,0:T(8,128)} %constant.2.clone.table_in), custom_call_target="tpu_custom_call" | custom-call | tf_op jit(solution)/shard_map/pallas_call | solution.py:352
  41.0 1.8 %copy.6 = bf16[128,1792]{1,0:T(8,128)(2,1)} copy(bf16[128,1792]{1,0:T(8,128)(2,1)} %shard_map.46) | data formatting | bytes 917504

commit v3 on v2

--- a/solution.py
+++ b/solution.py
@@ -39,7 +39,7 @@
 
 def kernel(
     shape, q_in, k_in, v_in, table_in, out,
-    q_raw, q_rot, kv, k_rot, table, table_next, table_far, peak, total, acc, o_buf,
+    q_raw, q_rot, kv, k_rot, s_buf, w_buf, table, table_next, table_far, peak, total, acc, o_buf,
     local_sem, pair_send, pair_recv, slot_recv, chain_send, flat_send, relay_send,
     out_local, out_send, out_recv,
 ):
@@ -210,37 +210,46 @@
             cosine, sine = factors(table[tile, :])
             k_rot[i * rows : (i + 1) * rows, :] = turned(kv[0, d, tile, :], cosine, sine)
 
-        def head(c, inner):
-            scores = lax.dot_general(
+        def score(c):
+            s_buf[c % 2] = lax.dot_general(
                 q_rot[version, c], k_rot[...], (((1,), (1,)), ((), ())),
                 preferred_element_type=jnp.float32,
             )
-            if causal:
-                row = b * rows + lax.broadcasted_iota(jnp.int32, scores.shape, 0)
-                key = lax.broadcasted_iota(jnp.int32, scores.shape, 1)
-                scores = jnp.where(row >= key, scores, -1e30)
-            new = jnp.max(scores, axis=1, keepdims=True) * SCALE
-            if not causal:
-                old = peak[c]
-                new = jnp.maximum(old, new)
-                fade = jnp.exp2(old - new)
-                peak[c] = new
-                new = new[:, :1]
-            else:
-                peak[c] = jnp.broadcast_to(new, (rows, HEAD_SIZE))
-            weights = jnp.exp2(scores * SCALE - new)
-            part = weights[:, :HEAD_SIZE]
-            for i in range(1, span // HEAD_SIZE):
-                part = part + weights[:, i * HEAD_SIZE : (i + 1) * HEAD_SIZE]
+
+        score(0)
+        for c in range(CLUSTER):
+            if c + 1 < CLUSTER:
+                score(c + 1)
+            for start in range(0, rows, 64):
+                sub = slice(start, start + 64)
+                scores = s_buf[c % 2, sub, :]
+                if causal:
+                    row = b * rows + start + lax.broadcasted_iota(jnp.int32, scores.shape, 0)
+                    key = lax.broadcasted_iota(jnp.int32, scores.shape, 1)
+                    scores = jnp.where(row >= key, scores, -1e30)
+                new = jnp.max(scores, axis=1, keepdims=True) * SCALE
+                if not causal:
+                    old = peak[c, sub, :]
+                    new = jnp.maximum(old, new)
+                    fade = jnp.exp2(old - new)
+                    peak[c, sub, :] = new
+                    new = new[:, :1]
+                else:
+                    peak[c, sub, :] = jnp.broadcast_to(new, (64, HEAD_SIZE))
+                weights = jnp.exp2(scores * SCALE - new)
+                part = weights[:, :HEAD_SIZE]
+                for i in range(1, span // HEAD_SIZE):
+                    part = part + weights[:, i * HEAD_SIZE : (i + 1) * HEAD_SIZE]
+                if causal:
+                    total[c, sub, :] = part
+                else:
+                    total[c, sub, :] = total[c, sub, :] * fade + part
+                    acc[c, sub, :] = acc[c, sub, :] * fade
+                w_buf[c % 2, sub, :] = weights.astype(jnp.bfloat16)
             product = jnp.dot(
-                weights.astype(jnp.bfloat16), kv[1, d, where, :],
-                preferred_element_type=jnp.float32,
+                w_buf[c % 2], kv[1, d, where, :], preferred_element_type=jnp.float32
             )
-            total[c] = part if causal else total[c] * fade + part
-            acc[c] = product if causal else acc[c] * fade + product
-            return inner
-
-        lax.fori_loop(0, CLUSTER, head, 0, unroll=UNROLL)
+            acc[c] = product if causal else acc[c] + product
 
     column(0, True)
     for copy in local[2:]:
@@ -359,6 +368,8 @@
             pltpu.VMEM((3, CLUSTER, rows, HEAD_SIZE), jnp.bfloat16),
             pltpu.VMEM((2, BLOCKS, length, HEAD_SIZE), jnp.bfloat16),
             pltpu.VMEM((span, HEAD_SIZE), jnp.bfloat16),
+            pltpu.VMEM((2, rows, span), jnp.float32),
+            pltpu.VMEM((2, rows, span), jnp.bfloat16),
             pltpu.VMEM((length, HEAD_SIZE), jnp.float32),
             pltpu.VMEM((rows, HEAD_SIZE), jnp.float32),
             pltpu.VMEM((8, HEAD_SIZE), jnp.float32),

time: 43 us -> 39.1 us (0.909)
  Pallas kernels: 41 us -> 37 us
    pallas_call x1, Pallas kernels: 41 us -> 37 us  [on_device(): pl.pallas_call(functools.partial(kernel, shape), out_shape=jax.ShapeDtype...]
where the time goes in v3:
time: 39.1 us; the launch traced here: 38.8 us
  Pallas kernels  37 us (95%)
  local copies, waits for them, and re-layouts  1.82 us (5%)
    pallas_call x1, Pallas kernels, on_device(): pl.pallas_call(functools.partial(kernel, shape), out_shape=jax.ShapeDtype...  37 us
    unnamed x1, local copies, waits for them, and re-layouts  1.82 us

profile of v3, /device:TPU:25, one launch (start us, length us, event | category | flops | bytes accessed | tf_op | source)
XLA Modules:
  0.0 38.8 jit_solution(15491205542394814525)
XLA Ops:
  0.0 37.0 %shard_map.46 = bf16[128,1792]{1,0:T(8,128)(2,1)} custom-call(bf16[128,1792]{1,0:T(8,128)(2,1)} %q_in.1, bf16[128,256]{1,0:T(8,128)(2,1)} %k_in.1, bf16[128,256]{1,0:T(8,128)(2,1)} %v_in.1, f32[2048,128]{1,0:T(8,128)} %constant.2.clone.table_in), custom_call_target="tpu_custom_call" | custom-call | tf_op jit(solution)/shard_map/pallas_call | solution.py:361
  37.0 1.8 %copy.6 = bf16[128,1792]{1,0:T(8,128)(2,1)} copy(bf16[128,1792]{1,0:T(8,128)(2,1)} %shard_map.46) | data formatting | bytes 917504
